TPU v7x, 32 devices: a whole 2x2x4 slice. The times are simulated.
32 devices in a mesh: mem: 4 (over z), reg: 8 (over y, x, core).
Axes of the slice: x: 2, y: 2, z: 4, core: 2. Of those that a mesh axis runs over, the one named last changes fastest.
Arguments:
- member_values: float32 [40, 32768], P('mem', 'reg'), may hold values from -6 to 6
- obs_value: float32 [32768], P('reg'), may hold values from -6 to 6
- obs_weight: float32 [32768], P('reg'), may hold values from 0.25 to 4
- obs_cell: int32 [32768], P('reg'), may hold values from -1 to 15359, as said below
Outputs:
- deviation: float32 [40, 15360], P('mem', 'reg')
- departure: float32 [15360], P('reg')
- variance: float32 [15360], P('reg')
- error_variance: float32 [15360], P('reg')
- obs_total: int32 [15360], P('reg')
Inputs may be any that keep to these rules, and one draw needn't show every extreme that they name: `obs_cell`: cell c is owned by region c // 1920. The 4096 slots of one region are 8 blocks of 512 slots, block r holding only cells owned by region r, live slots first and -1 in the empty ones. Every block has at least 128 live slots; one owner's block is full in every region.
All inputs are finite; a program needn't handle non-finite values.
Results may differ from a plain program's by a relative error of at most 0.0003.
Values sent between devices are 32-bit elements; how exact they have to be, the bound alone decides.
No kernel may reach another device: no remote copies, remote signals or barrier semaphores. Data moves between devices by JAX's collectives and lax.ppermute only.
A program may use at most 64 MiB of HBM per device.

v0:
```python
import jax
import jax.numpy as jnp
from jax import lax
from jax.sharding import PartitionSpec as P

CELL_DEV = 1920


def shards(member_values, obs_value, obs_weight, obs_cell):
    regions = lax.axis_size("reg")
    groups = lax.axis_size("mem")
    obs_dev = obs_cell.shape[0]
    capacity = obs_dev // regions
    live = obs_cell >= 0
    weight = jnp.where(live, obs_weight, jnp.float32(0.0))
    local_cell = jnp.where(live, obs_cell % CELL_DEV, 0).astype(jnp.float32)
    weighted_members = member_values * weight[None, :]
    meta_rows = jnp.stack([weight * obs_value, weight, local_cell])
    member_buffer = weighted_members.reshape(weighted_members.shape[0], regions, capacity)
    meta_buffer = meta_rows.reshape(3, regions, capacity)
    payload = jnp.concatenate([member_buffer, meta_buffer], 0)
    received = lax.all_to_all(payload, "reg", split_axis=1, concat_axis=1, tiled=True)
    received = received.reshape(received.shape[0], -1)
    members_in = received[:-3]
    meta_in = received[-3:]
    cell_in = meta_in[2].astype(jnp.int32)
    filled_flag = (meta_in[1] > 0).astype(jnp.float32)
    columns = jnp.concatenate([members_in, meta_in[:2], filled_flag[None, :]], 0)
    total_rows = columns.shape[1]
    block_rows = 1024
    column_blocks = columns.reshape(
        columns.shape[0], total_rows // block_rows, block_rows
    ).transpose(1, 0, 2)
    cell_blocks = cell_in.reshape(total_rows // block_rows, block_rows)
    cell_range = jnp.arange(CELL_DEV, dtype=jnp.int32)

    def add_block(carry, inputs):
        block_columns, block_cells = inputs
        one_hot = (block_cells[:, None] == cell_range[None, :]).astype(jnp.float32)
        return (
            carry
            + jnp.dot(
                block_columns,
                one_hot,
                precision=lax.Precision.HIGHEST,
                preferred_element_type=jnp.float32,
            ),
            None,
        )

    start_sums = jnp.zeros((columns.shape[0], CELL_DEV), jnp.float32)
    cell_sums, _ = lax.scan(add_block, start_sums, (column_blocks, cell_blocks))
    counted = cell_sums[-1]
    filled = counted > 0
    weight_total = jnp.where(filled, cell_sums[-2], jnp.float32(1.0))
    superob = cell_sums[:-3] / weight_total[None, :]
    observed_mean = cell_sums[-3] / weight_total
    ensemble = member_values.shape[0] * groups
    moment_one, moment_two = lax.psum((jnp.sum(superob, 0), jnp.sum(superob * superob, 0)), "mem")
    ens_mean = moment_one / ensemble
    deviation = superob - ens_mean[None, :]
    variance = (moment_two - moment_one * ens_mean) / (ensemble - 1)
    departure = observed_mean - ens_mean
    error_variance = jnp.where(filled, 1.0 / weight_total, jnp.float32(0.0))
    return (deviation, departure, variance, error_variance, counted.astype(jnp.int32))


def solution(mesh):
    return jax.shard_map(
        shards,
        mesh=mesh,
        in_specs=(P("mem", "reg"), P("reg"), P("reg"), P("reg")),
        out_specs=(P("mem", "reg"), P("reg"), P("reg"), P("reg"), P("reg")),
        check_vma=False,
    )
```

profile of v0, /device:TPU:0, one launch (start us, length us, event | category | flops | bytes accessed | tf_op | source)
XLA Modules:
  0.0 48.5 jit_solution(72465091545235863)
XLA Ops:
  0.6 0.7 %fusion.6 = f32[4096]{0:T(1024)S(1)} fusion(s32[4096]{0:T(1024)} %param.9), kind=kLoop, calls=%fused_computation.17 | loop fusion | flops 36864 | bytes 32768 | tf_op jit(solution)/shard_map/convert_element_type | solution.py:16
  1.4 0.8 %fusion.11 = (f32[4096]{0:T(1024)S(1)}, f32[4096]{0:T(1024)S(1)}) fusion(f32[4096]{0:T(1024)} %param.7, f32[4096]{0:T(1024)} %param.8, s32[4096]{0:T(1024)} %param.9), kind=kLoop, calls=%fused_computation.34 | loop fusion | flops 12288 | bytes 81920 | tf_op jit(solution)/shard_map/mul | solution.py:18
  2.1 1.0 %broadcast_multiply_fusion = f32[10,4096]{1,0:T(8,128)S(1)} fusion(f32[10,4096]{1,0:T(8,128)} %param.6, f32[4096]{0:T(1024)S(1)} %get-tuple-element.78), kind=kLoop, calls=%fused_computation.10 | loop fusion | flops 40960 | bytes 344064 | tf_op jit(solution)/shard_map/mul | solution.py:17
  3.1 0.2 copy.18
  3.3 0.8 %copy.13 = f32[13,8,512]{2,0,1:T(8,128)} copy(f32[13,8,512]{2,1,0:T(8,128)S(1)} %pad_maximum_fusion) | data formatting | bytes 425984 | tf_op jit(solution)/shard_map/concatenate | solution.py:21
  4.2 5.2 %all-to-all-start = ((f32[13,8,512]{2,0,1:T(8,128)}), f32[13,8,512]{2,0,1:T(8,128)S(1)}, u32[]{:S(2)}, u32[]{:S(2)}) async-start(f32[13,8,512]{2,0,1:T(8,128)} %copy.13), calls=%async_computation | async-start | bytes 524288 | tf_op jit(solution)/shard_map/all_to_all | solution.py:22
  9.4 6.9 %all-to-all-done = f32[13,8,512]{2,0,1:T(8,128)S(1)} async-done(((f32[13,8,512]{2,0,1:T(8,128)}), f32[13,8,512]{2,0,1:T(8,128)S(1)}, u32[]{:S(2)}, u32[]{:S(2)}) %all-to-all-start) | async-done | bytes 213024 | tf_op jit(solution)/shard_map/all_to_all | solution.py:22
  16.3 0.1 copy.14
  16.4 0.1 concatenate.14
  16.5 0.1 fusion.7
  16.6 0.1 fusion.8
  16.7 0.1 maximum_bitcast_fusion
  16.8 10.7 %while.11 = (s32[]{:T(128)}, f32[13,1920]{1,0:T(8,128)S(1)}, f32[4,13,1024]{2,0,1:T(4,128)S(1)}, s32[4,1024]{1,0:T(4,128)S(1)}, s32[]{:T(128)}, /*index=5*/s32[]{:T(128)}) while((s32[]{:T(128)}, f32[13,1920]{1,0:T(8,128)S(1)}, f32[4,13,1024]{2,0,1:T(4,128)S(1)}, s32[4,1024]{1,0:T(4,128)S(1)}, s32[]{:T(128)}, ...), condition=%wide.region_1.2_spmd.clone, body=%wide.region_0.1_spmd.clone.sunk | while | flops 308724480 | bytes 371799 | solution.py:52
  16.8 0.1 constant_dynamic-slice_fusion.5
  16.9 2.6 %fusion.13 = f32[13,1920]{1,0:T(8,128)S(1)} fusion(s32[1024]{0:T(1024)S(1)} %bitcast.17, f32[13,1920]{1,0:T(8,128)S(1)} %get-tuple-element.115, f32[1,13,1024]{2,0,1:T(1,128)S(1)} %constant_dynamic-slice_fusion.5, pred[]{:T(512)S(6)} %compare.3), kind=kOutput, calls=%fused_computation.4.clone.1 | convolution fusion | flops 308724480 | bytes 257025 | tf_op jit(solution)/shard_map/while/body/eval_jaxpr/dot_general | solution.py:42
  19.4 0.1 constant_dynamic-slice_fusion.5
  19.5 2.6 %fusion.13 = f32[13,1920]{1,0:T(8,128)S(1)} fusion(s32[1024]{0:T(1024)S(1)} %bitcast.17, f32[13,1920]{1,0:T(8,128)S(1)} %get-tuple-element.115, f32[1,13,1024]{2,0,1:T(1,128)S(1)} %constant_dynamic-slice_fusion.5, pred[]{:T(512)S(6)} %compare.3), kind=kOutput, calls=%fused_computation.4.clone.1 | convolution fusion | flops 308724480 | bytes 257025 | tf_op jit(solution)/shard_map/while/body/eval_jaxpr/dot_general | solution.py:42
  22.1 0.1 constant_dynamic-slice_fusion.5
  22.2 2.6 %fusion.13 = f32[13,1920]{1,0:T(8,128)S(1)} fusion(s32[1024]{0:T(1024)S(1)} %bitcast.17, f32[13,1920]{1,0:T(8,128)S(1)} %get-tuple-element.115, f32[1,13,1024]{2,0,1:T(1,128)S(1)} %constant_dynamic-slice_fusion.5, pred[]{:T(512)S(6)} %compare.3), kind=kOutput, calls=%fused_computation.4.clone.1 | convolution fusion | flops 308724480 | bytes 257025 | tf_op jit(solution)/shard_map/while/body/eval_jaxpr/dot_general | solution.py:42
  24.8 0.1 constant_dynamic-slice_fusion.5
  24.9 2.6 %fusion.13 = f32[13,1920]{1,0:T(8,128)S(1)} fusion(s32[1024]{0:T(1024)S(1)} %bitcast.17, f32[13,1920]{1,0:T(8,128)S(1)} %get-tuple-element.115, f32[1,13,1024]{2,0,1:T(1,128)S(1)} %constant_dynamic-slice_fusion.5, pred[]{:T(512)S(6)} %compare.3), kind=kOutput, calls=%fused_computation.4.clone.1 | convolution fusion | flops 308724480 | bytes 257025 | tf_op jit(solution)/shard_map/while/body/eval_jaxpr/dot_general | solution.py:42
  27.5 0.1 slice_reduce_fusion.1
  27.6 0.6 %convert_reduce_fusion = s32[1920]{0:T(1024)} fusion(f32[13,1920]{1,0:T(8,128)S(1)} %get-tuple-element.32), kind=kLoop, calls=%fused_computation.29 | loop fusion | flops 1920 | bytes 15360 | tf_op jit(solution)/shard_map/convert_element_type | solution.py:65
  28.2 0.1 multiply_reduce_fusion
  28.3 19.0 %all-reduce = (f32[1920]{0:T(1024)S(1)}, f32[1920]{0:T(1024)S(1)}) all-reduce(f32[1920]{0:T(1024)S(1)} %get-tuple-element.63, f32[1920]{0:T(1024)S(1)} %get-tuple-element.62), channel_id=1, replica_groups=mesh['mem'=4,'reg'=8] {'mem'}, use_global_device_ids=true, to_apply=%region_3.4 | all-reduce | flops 3840 | bytes 30720 | tf_op jit(solution)/shard_map/psum | solution.py:59
  47.3 0.6 %divide_select_fusion = (f32[1920]{0:T(1024)}, f32[1920]{0:T(1024)}, f32[1920]{0:T(1024)}, f32[1920]{0:T(1024)S(1)}) fusion(pred[1920]{0:T(1024)(128)(4,1)S(1)} %compare_reduce_fusion, f32[1920]{0:T(1024)S(1)} %get-tuple-element.64, f32[1920]{0:T(1024)S(1)} %get-tuple-element.75, f32[1920]{0:T(1024)S(1)} %get-tuple-element.65, f32[1920]{0:T(1024)S(1)} %get-tuple-element.76), kind=kLoop, calls=%fused_computation.23 | loop fusion | flops 17280 | bytes 63360 | tf_op jit(solution)/shard_map/jit(_where)/select_n | solution.py:64
  47.9 0.7 %broadcast_subtract_fusion = f32[10,1920]{1,0:T(8,128)} fusion(f32[1920]{0:T(1024)S(1)} %get-tuple-element.82, f32[1920]{0:T(1024)S(1)} %get-tuple-element.66, f32[13,1920]{1,0:T(8,128)S(1)} %get-tuple-element.32), kind=kLoop, calls=%fused_computation.14 | loop fusion | flops 38400 | bytes 168960 | tf_op jit(solution)/shard_map/sub | solution.py:61
  (16 shorter events, 0.2 us)
Async XLA Ops:
  4.2 12.1 %all-to-all-start = ((f32[13,8,512]{2,0,1:T(8,128)}), f32[13,8,512]{2,0,1:T(8,128)S(1)}, u32[]{:S(2)}, u32[]{:S(2)}) async-start(f32[13,8,512]{2,0,1:T(8,128)} %copy.13), calls=%async_computation | async-start | bytes 524288 | tf_op jit(solution)/shard_map/all_to_all | solution.py:22
where the time goes:
time: 49 us; the launch traced here: 48.5 us
  blocking collectives  19 us (39%)
  matrix products  10.3 us (21%)
  waiting for transfers between devices  6.9 us (14%)
  starting transfers between devices  5.2 us (11%)
  other arithmetic  4.73 us (10%)
  local copies, waits for them, and re-layouts  1.52 us (3%)
  between operations  0.77 us (2%)
    psum x1, blocking collectives, shards(): lax.psum((jnp.sum(superob, 0), jnp.sum(superob * superob, 0)), 'mem')  19 us
    dot_general x4, matrix products, add_block(): jnp.dot(block_columns, one_hot, precision=lax.Precision.HIGHEST, preferre...  10.3 us
    all_to_all x1, waiting for transfers between devices, shards(): lax.all_to_all(payload, 'reg', split_axis=1, concat_axis=1, tiled=True)  6.9 us
    all_to_all x1, starting transfers between devices, shards(): lax.all_to_all(payload, 'reg', split_axis=1, concat_axis=1, tiled=True)  5.2 us
  transfers between devices with their start and end apart: 1, of which 1 were waited for; matrix products, arithmetic and copies ran while one was open for 0% of the time, Pallas kernels for 0%

commit v1 on v0

--- a/solution.py
+++ b/solution.py
@@ -19,7 +19,10 @@
     member_buffer = weighted_members.reshape(weighted_members.shape[0], regions, capacity)
     meta_buffer = meta_rows.reshape(3, regions, capacity)
     payload = jnp.concatenate([member_buffer, meta_buffer], 0)
-    received = lax.all_to_all(payload, "reg", split_axis=1, concat_axis=1, tiled=True)
+    received = jnp.concatenate(
+        lax.all_to_all(jnp.stack(jnp.split(payload, lax.axis_size("reg"), axis=1)), "reg", 0, 0),
+        axis=1,
+    )
     received = received.reshape(received.shape[0], -1)
     members_in = received[:-3]
     meta_in = received[-3:]

time: 49 us -> 52.6 us (1.073)
  local copies, waits for them, and re-layouts: 1.52 us -> 5.67 us
    unnamed x1 -> x11, local copies, waits for them, and re-layouts: 0.16 us -> 4.57 us
    concatenate x1, local copies, waits for them, and re-layouts: 0.82 us -> 0.01 us  [shards(): payload = jnp.concatenate([member_buffer, meta_buffer], 0)]
    another operation x0 -> x1, local copies, waits for them, and re-layouts: none -> 0.64 us  [shards(): jnp.stack(jnp.split(payload, lax.axis_size('reg'), axis=1))]
    all_to_all x1, waiting for transfers between devices: 6.9 us -> 6.38 us  [shards(): lax.all_to_all(jnp.stack(jnp.split(payload, lax.axis_size('reg'), axis=1)...]
where the time goes in v1:
time: 52.6 us; the launch traced here: 52.2 us
  blocking collectives  19 us (36%)
  matrix products  10.3 us (20%)
  waiting for transfers between devices  6.38 us (12%)
  local copies, waits for them, and re-layouts  5.67 us (11%)
  starting transfers between devices  5.2 us (10%)
  other arithmetic  4.69 us (9%)
  between operations  0.8 us (2%)
    psum x1, blocking collectives, shards(): lax.psum((jnp.sum(superob, 0), jnp.sum(superob * superob, 0)), 'mem')  19 us
    dot_general x4, matrix products, add_block(): jnp.dot(block_columns, one_hot, precision=lax.Precision.HIGHEST, preferre...  10.3 us
    all_to_all x1, waiting for transfers between devices, shards(): lax.all_to_all(jnp.stack(jnp.split(payload, lax.axis_size('reg'), axis=1)...  6.38 us
    all_to_all x1, starting transfers between devices, shards(): lax.all_to_all(jnp.stack(jnp.split(payload, lax.axis_size('reg'), axis=1)...  5.2 us
    unnamed x11, local copies, waits for them, and re-layouts  4.57 us
  transfers between devices with their start and end apart: 1, of which 1 were waited for; matrix products, arithmetic and copies ran while one was open for 0% of the time, Pallas kernels for 0%

profile of v1, /device:TPU:0, one launch (start us, length us, event | category | flops | bytes accessed | tf_op | source)
XLA Modules:
  0.0 52.2 jit_solution(6257856865962109668)
XLA Ops:
  0.6 0.7 %fusion.14 = f32[4096]{0:T(1024)S(1)} fusion(s32[4096]{0:T(1024)} %param.9), kind=kLoop, calls=%fused_computation.36 | loop fusion | flops 36864 | bytes 32768 | tf_op jit(solution)/shard_map/convert_element_type | solution.py:16
  1.4 0.8 %fusion.19 = (f32[4096]{0:T(1024)S(1)}, f32[4096]{0:T(1024)S(1)}) fusion(f32[4096]{0:T(1024)} %param.7, f32[4096]{0:T(1024)} %param.8, s32[4096]{0:T(1024)} %param.9), kind=kLoop, calls=%fused_computation.53 | loop fusion | flops 12288 | bytes 81920 | tf_op jit(solution)/shard_map/mul | solution.py:18
  2.1 1.0 %broadcast_multiply_fusion = f32[10,4096]{1,0:T(8,128)S(1)} fusion(f32[10,4096]{1,0:T(8,128)} %param.6, f32[4096]{0:T(1024)S(1)} %get-tuple-element.82), kind=kLoop, calls=%fused_computation.10 | loop fusion | flops 40960 | bytes 344064 | tf_op jit(solution)/shard_map/mul | solution.py:17
  3.1 0.2 copy.35
  3.4 0.6 %fusion.12 = f32[8,13,1,512]{3,2,1,0:T(1,128)} fusion(f32[13,8,512]{2,1,0:T(8,128)S(1)} %constant_dynamic-update-slice_fusion), kind=kLoop, calls=%fused_computation.30 | loop fusion | bytes 53248
  4.0 0.6 %fusion.11 = f32[8,13,1,512]{3,2,1,0:T(1,128)} fusion(f32[8,13,1,512]{3,2,1,0:T(1,128)} %fusion.12, f32[13,8,512]{2,1,0:T(8,128)S(1)} %constant_dynamic-update-slice_fusion), kind=kLoop, calls=%fused_computation.28 | loop fusion | bytes 53248
  4.6 0.6 %fusion.10 = f32[8,13,1,512]{3,2,1,0:T(1,128)} fusion(f32[8,13,1,512]{3,2,1,0:T(1,128)} %fusion.11, f32[13,8,512]{2,1,0:T(8,128)S(1)} %constant_dynamic-update-slice_fusion), kind=kLoop, calls=%fused_computation.26 | loop fusion | bytes 53248
  5.2 0.6 %fusion.9 = f32[8,13,1,512]{3,2,1,0:T(1,128)} fusion(f32[8,13,1,512]{3,2,1,0:T(1,128)} %fusion.10, f32[13,8,512]{2,1,0:T(8,128)S(1)} %constant_dynamic-update-slice_fusion), kind=kLoop, calls=%fused_computation.24 | loop fusion | bytes 53248
  5.9 0.6 %fusion.8 = f32[8,13,1,512]{3,2,1,0:T(1,128)} fusion(f32[8,13,1,512]{3,2,1,0:T(1,128)} %fusion.9, f32[13,8,512]{2,1,0:T(8,128)S(1)} %constant_dynamic-update-slice_fusion), kind=kLoop, calls=%fused_computation.22 | loop fusion | bytes 53248
  6.5 0.6 %fusion.7 = f32[8,13,1,512]{3,2,1,0:T(1,128)} fusion(f32[8,13,1,512]{3,2,1,0:T(1,128)} %fusion.8, f32[13,8,512]{2,1,0:T(8,128)S(1)} %constant_dynamic-update-slice_fusion), kind=kLoop, calls=%fused_computation.20 | loop fusion | bytes 53248
  7.1 0.6 %fusion.6 = f32[8,13,1,512]{3,2,1,0:T(1,128)} fusion(f32[8,13,1,512]{3,2,1,0:T(1,128)} %fusion.7, f32[13,8,512]{2,1,0:T(8,128)S(1)} %constant_dynamic-update-slice_fusion), kind=kLoop, calls=%fused_computation.18 | loop fusion | bytes 53248
  7.7 0.6 %fusion.5 = f32[8,13,1,512]{3,2,1,0:T(1,128)} fusion(f32[8,13,1,512]{3,2,1,0:T(1,128)} %fusion.6, f32[13,8,512]{2,1,0:T(8,128)S(1)} %constant_dynamic-update-slice_fusion), kind=kLoop, calls=%fused_computation.16 | loop fusion | bytes 53248 | tf_op jit(solution)/shard_map/stack | solution.py:23
  8.4 5.2 %all-to-all-start = ((f32[8,13,1,512]{3,2,1,0:T(1,128)}), f32[8,13,1,512]{3,2,1,0:T(1,128)S(1)}, u32[]{:S(2)}, u32[]{:S(2)}) async-start(f32[8,13,1,512]{3,2,1,0:T(1,128)} %fusion.5), calls=%async_computation | async-start | bytes 425984 | tf_op jit(solution)/shard_map/all_to_all | solution.py:23
  13.6 6.4 %all-to-all-done = f32[8,13,1,512]{3,2,1,0:T(1,128)S(1)} async-done(((f32[8,13,1,512]{3,2,1,0:T(1,128)}), f32[8,13,1,512]{3,2,1,0:T(1,128)S(1)}, u32[]{:S(2)}, u32[]{:S(2)}) %all-to-all-start) | async-done | bytes 213024 | tf_op jit(solution)/shard_map/all_to_all | solution.py:23
  20.1 0.1 concatenate.14
  20.3 0.1 maximum_bitcast_fusion
  20.4 10.7 %while.11 = (s32[]{:T(128)}, f32[13,1920]{1,0:T(8,128)S(1)}, f32[4,13,1024]{2,0,1:T(4,128)S(1)}, s32[4,1024]{1,0:T(4,128)S(1)}, s32[]{:T(128)}, /*index=5*/s32[]{:T(128)}) while((s32[]{:T(128)}, f32[13,1920]{1,0:T(8,128)S(1)}, f32[4,13,1024]{2,0,1:T(4,128)S(1)}, s32[4,1024]{1,0:T(4,128)S(1)}, s32[]{:T(128)}, ...), condition=%wide.region_1.2_spmd.clone, body=%wide.region_0.1_spmd.clone.sunk | while | flops 308724480 | bytes 371799 | solution.py:55
  20.4 0.1 constant_dynamic-slice_fusion.5
  20.5 2.6 %fusion.21 = f32[13,1920]{1,0:T(8,128)S(1)} fusion(s32[1024]{0:T(1024)S(1)} %bitcast.60, f32[13,1920]{1,0:T(8,128)S(1)} %get-tuple-element.119, f32[1,13,1024]{2,0,1:T(1,128)S(1)} %constant_dynamic-slice_fusion.5, pred[]{:T(512)S(6)} %compare.3), kind=kOutput, calls=%fused_computation.4.clone.1 | convolution fusion | flops 308724480 | bytes 257025 | tf_op jit(solution)/shard_map/while/body/eval_jaxpr/dot_general | solution.py:45
  23.1 0.1 constant_dynamic-slice_fusion.5
  23.1 2.6 %fusion.21 = f32[13,1920]{1,0:T(8,128)S(1)} fusion(s32[1024]{0:T(1024)S(1)} %bitcast.60, f32[13,1920]{1,0:T(8,128)S(1)} %get-tuple-element.119, f32[1,13,1024]{2,0,1:T(1,128)S(1)} %constant_dynamic-slice_fusion.5, pred[]{:T(512)S(6)} %compare.3), kind=kOutput, calls=%fused_computation.4.clone.1 | convolution fusion | flops 308724480 | bytes 257025 | tf_op jit(solution)/shard_map/while/body/eval_jaxpr/dot_general | solution.py:45
  25.7 0.1 constant_dynamic-slice_fusion.5
  25.8 2.6 %fusion.21 = f32[13,1920]{1,0:T(8,128)S(1)} fusion(s32[1024]{0:T(1024)S(1)} %bitcast.60, f32[13,1920]{1,0:T(8,128)S(1)} %get-tuple-element.119, f32[1,13,1024]{2,0,1:T(1,128)S(1)} %constant_dynamic-slice_fusion.5, pred[]{:T(512)S(6)} %compare.3), kind=kOutput, calls=%fused_computation.4.clone.1 | convolution fusion | flops 308724480 | bytes 257025 | tf_op jit(solution)/shard_map/while/body/eval_jaxpr/dot_general | solution.py:45
  28.4 0.1 constant_dynamic-slice_fusion.5
  28.5 2.6 %fusion.21 = f32[13,1920]{1,0:T(8,128)S(1)} fusion(s32[1024]{0:T(1024)S(1)} %bitcast.60, f32[13,1920]{1,0:T(8,128)S(1)} %get-tuple-element.119, f32[1,13,1024]{2,0,1:T(1,128)S(1)} %constant_dynamic-slice_fusion.5, pred[]{:T(512)S(6)} %compare.3), kind=kOutput, calls=%fused_computation.4.clone.1 | convolution fusion | flops 308724480 | bytes 257025 | tf_op jit(solution)/shard_map/while/body/eval_jaxpr/dot_general | solution.py:45
  31.1 0.1 slice_reduce_fusion.1
  31.2 0.6 %convert_reduce_fusion = s32[1920]{0:T(1024)} fusion(f32[13,1920]{1,0:T(8,128)S(1)} %get-tuple-element.32), kind=kLoop, calls=%fused_computation.48 | loop fusion | flops 1920 | bytes 15360 | tf_op jit(solution)/shard_map/convert_element_type | solution.py:68
  31.8 0.1 multiply_reduce_fusion
  31.9 19.0 %all-reduce = (f32[1920]{0:T(1024)S(1)}, f32[1920]{0:T(1024)S(1)}) all-reduce(f32[1920]{0:T(1024)S(1)} %get-tuple-element.67, f32[1920]{0:T(1024)S(1)} %get-tuple-element.66), channel_id=1, replica_groups=mesh['mem'=4,'reg'=8] {'mem'}, use_global_device_ids=true, to_apply=%region_3.4 | all-reduce | flops 3840 | bytes 30720 | tf_op jit(solution)/shard_map/psum | solution.py:62
  50.9 0.6 %divide_select_fusion = (f32[1920]{0:T(1024)}, f32[1920]{0:T(1024)}, f32[1920]{0:T(1024)}, f32[1920]{0:T(1024)S(1)}) fusion(pred[1920]{0:T(1024)(128)(4,1)S(1)} %compare_reduce_fusion, f32[1920]{0:T(1024)S(1)} %get-tuple-element.68, f32[1920]{0:T(1024)S(1)} %get-tuple-element.79, f32[1920]{0:T(1024)S(1)} %get-tuple-element.69, f32[1920]{0:T(1024)S(1)} %get-tuple-element.80), kind=kLoop, calls=%fused_computation.42 | loop fusion | flops 17280 | bytes 63360 | tf_op jit(solution)/shard_map/jit(_where)/select_n | solution.py:67
  51.5 0.7 %broadcast_subtract_fusion = f32[10,1920]{1,0:T(8,128)} fusion(f32[1920]{0:T(1024)S(1)} %get-tuple-element.86, f32[1920]{0:T(1024)S(1)} %get-tuple-element.70, f32[13,1920]{1,0:T(8,128)S(1)} %get-tuple-element.32), kind=kLoop, calls=%fused_computation.14 | loop fusion | flops 38400 | bytes 168960 | tf_op jit(solution)/shard_map/sub | solution.py:64
  (22 shorter events, 0.3 us)
Async XLA Ops:
  8.4 11.6 %all-to-all-start = ((f32[8,13,1,512]{3,2,1,0:T(1,128)}), f32[8,13,1,512]{3,2,1,0:T(1,128)S(1)}, u32[]{:S(2)}, u32[]{:S(2)}) async-start(f32[8,13,1,512]{3,2,1,0:T(1,128)} %fusion.5), calls=%async_computation | async-start | bytes 425984 | tf_op jit(solution)/shard_map/all_to_all | solution.py:23
